TPU v7x, 512 devices: a whole 4x8x8 slice. The times are simulated.
512 devices in a mesh: row: 32 (over y, x), col: 16 (over z, core).
Axes of the slice: x: 4, y: 8, z: 8, core: 2. Of those that a mesh axis runs over, the one named last changes fastest.
Arguments:
- pair_factors: float32 [12288, 1024], P(('row', 'col')), may hold values from -0.09375 to 0.09375
- k_prev: float32 [12288, 12288], P('row', 'col'), as said below
- energies: float32 [12288], P('row'), may hold values from 0.3 to 2
Outputs:
- casida: float32 [12288, 12288], P('row', 'col')
- vectors: float32 [12288, 8], P('row')
- images: float32 [12288, 8], P('row')
- tridiagonal: float32 [2, 8], replicated
Inputs may be any that keep to these rules, and one draw needn't show every extreme that they name: k_prev is exactly symmetric.
All inputs are finite; a program needn't handle non-finite values.
Results may differ from a plain program's by a relative error of at most 0.0003.
Values sent between devices are 32-bit elements; how exact they have to be, the bound alone decides.
A program may use at most 64 MiB of HBM per device.

v0:
```python
import jax
import jax.numpy as jnp
from jax import lax
from jax.sharding import Mesh
from jax.sharding import PartitionSpec as P

N = 12288
PC = 8
ROW = ("row_0", "row_1")
ROW_COL = ("row_0", "row_1", "col")


def laid_out(pieces, dim):
    pieces = jnp.moveaxis(pieces, 0, dim)
    shape = pieces.shape
    return pieces.reshape(*shape[:dim], shape[dim] * shape[dim + 1], *shape[dim + 2 :])


def sent_to_all(value, axis):
    copies = jnp.broadcast_to(value, (lax.axis_size(axis), *value.shape))
    return lax.all_to_all(copies, axis, split_axis=0, concat_axis=0, tiled=True)


def gathered_copies(value, axis, dim):
    return laid_out(sent_to_all(value, axis), dim)


def spread(value, axes, root):
    value = jnp.where(lax.axis_index(axes) == root, value, jnp.zeros_like(value))
    for axis in axes:
        value = lax.psum(value, axis)
    return value


def picked(value, axis, root):
    return lax.dynamic_index_in_dim(lax.all_gather(value, axis), root, 0, keepdims=False)


def over_copies(value, axis):
    everything = sent_to_all(value, axis)
    return jnp.sum(everything, axis=0)


def packed_total(arrays, axis):
    flat, at, outs = (jnp.concatenate([a.reshape(-1) for a in arrays]), 0, [])
    so_far = over_copies(flat, axis)
    for a in arrays:
        outs.append(so_far[at : at + a.size].reshape(a.shape))
        at += a.size
    return tuple(outs)


def shards(pair_factors, k_prev, energies):
    rows_here, cols_here = k_prev.shape
    per_col = lax.axis_size(ROW) // lax.axis_size("col")
    row_index = lax.axis_index(ROW)
    col_index = lax.axis_index("col")
    left_rows = gathered_copies(pair_factors, "col", 0)
    right_parts = []
    for offset in range(per_col):
        right_parts.append(spread(left_rows, ROW, per_col * col_index + offset))
    right_rows = jnp.concatenate(right_parts, axis=0)
    total = lax.dot_general(
        left_rows,
        right_rows,
        (((1,), (1,)), ((), ())),
        precision=lax.Precision.HIGHEST,
        preferred_element_type=jnp.float32,
    )
    global_rows = row_index * rows_here + jnp.arange(rows_here, dtype=jnp.int32)
    global_cols = col_index * cols_here + jnp.arange(cols_here, dtype=jnp.int32)
    on_diagonal = global_rows[:, None] == global_cols[None, :]
    casida = 4.0 * (k_prev + total) + jnp.where(on_diagonal, energies[:, None], 0.0)
    col_ids = jnp.arange(PC, dtype=jnp.int32)
    scale = jnp.sqrt(jnp.float32(N))
    diag_list = []
    sub_list = []
    head_ids = jnp.arange(PC + 1, dtype=jnp.int32)
    upper = jnp.zeros((rows_here, PC), jnp.float32)
    lower = jnp.zeros((rows_here, PC), jnp.float32)
    upper_head = jnp.zeros((PC + 1, PC), jnp.float32)
    lower_head = jnp.zeros((PC + 1, PC), jnp.float32)
    on_first = row_index == 0
    for column_at in range(PC):
        raw_column = picked(casida[:, column_at], "col", 0)
        column = (
            raw_column
            - jnp.dot(upper, lower_head[column_at], precision=lax.Precision.HIGHEST)
            - jnp.dot(lower, upper_head[column_at], precision=lax.Precision.HIGHEST)
        )
        below = jnp.where(global_rows > column_at, column, 0.0)
        head_part = jnp.where(on_first, column[: PC + 1], 0.0)
        sigma, head, upper_proj, lower_proj = packed_total(
            (
                jnp.sum(below * below),
                head_part,
                jnp.dot(upper.T, below, precision=lax.Precision.HIGHEST),
                jnp.dot(lower.T, below, precision=lax.Precision.HIGHEST),
            ),
            ROW,
        )
        diag_list.append(head[column_at])
        lead = head[column_at + 1]
        root = jnp.sqrt(sigma)
        alpha = jnp.where(lead >= 0, -root, root)
        length = jnp.sqrt(jnp.maximum(2.0 * (sigma + jnp.abs(lead) * root), 1.0))
        unit = (below - alpha * (global_rows == column_at + 1).astype(jnp.float32)) / length
        unit_head = (
            jnp.where(head_ids > column_at, head, 0.0)
            - alpha * (head_ids == column_at + 1).astype(jnp.float32)
        ) / length
        upper_unit = (upper_proj - alpha * upper_head[column_at + 1]) / length
        lower_unit = (lower_proj - alpha * lower_head[column_at + 1]) / length
        partial_cols = jnp.dot(unit, casida, precision=lax.Precision.HIGHEST)
        summed_cols = over_copies(partial_cols, ROW)
        owner_block = picked(summed_cols, "col", row_index // per_col)
        image = lax.dynamic_slice_in_dim(owner_block, row_index % per_col * rows_here, rows_here, 0)
        image = (
            image
            - jnp.dot(upper, lower_unit, precision=lax.Precision.HIGHEST)
            - jnp.dot(lower, upper_unit, precision=lax.Precision.HIGHEST)
        )
        image = 2.0 * image
        image_head_part = jnp.where(on_first, image[: PC + 1], 0.0)
        product, image_head = packed_total((jnp.sum(image * unit), image_head_part), ROW)
        partner = image - product * unit
        partner_head = image_head - product * unit_head
        pick = (col_ids == column_at).astype(jnp.float32)[None, :]
        upper = upper + unit[:, None] * pick
        lower = lower + partner[:, None] * pick
        upper_head = upper_head + unit_head[:, None] * pick
        lower_head = lower_head + partner_head[:, None] * pick
        sub_list.append(alpha)
    tridiagonal = jnp.stack([jnp.stack(diag_list), jnp.stack(sub_list)])
    return (casida, scale * upper, scale * lower, tridiagonal)


def solution(mesh):
    split = Mesh(mesh.devices.reshape(8, 4, mesh.shape["col"]), ("row_0", "row_1", "col"))
    in_specs = (P(ROW_COL, None), P(ROW, "col"), P(ROW))
    out_specs = (P(ROW, "col"), P(ROW, None), P(ROW, None), P())
    return jax.shard_map(
        shards, mesh=split, in_specs=in_specs, out_specs=out_specs, check_vma=False
    )
```

profile of v0, /device:TPU:1, one launch (start us, length us, event | category | flops | bytes accessed | tf_op | source)
XLA Modules:
  0.0 898.8 jit_solution(7743463168844762544)
XLA Ops:
  9.4 11.8 %all-to-all-start = ((f32[16,24,1024]{2,1,0:T(8,128)}), f32[16,24,1024]{2,1,0:T(8,128)S(1)}, u32[]{:S(2)}, u32[]{:S(2)}) async-start(f32[16,24,1024]{2,1,0:T(8,128)} %broadcast_in_dim.166), calls=%async_computation | async-start | bytes 3145728 | tf_op jit(solution)/shard_map/all_to_all | solution.py:21
  21.3 38.5 %all-to-all-done = f32[16,24,1024]{2,1,0:T(8,128)S(1)} async-done(((f32[16,24,1024]{2,1,0:T(8,128)}), f32[16,24,1024]{2,1,0:T(8,128)S(1)}, u32[]{:S(2)}, u32[]{:S(2)}) %all-to-all-start) | async-done | bytes 1572896 | tf_op jit(solution)/shard_map/all_to_all | solution.py:21
  61.8 93.9 %all-reduce.5.cloned.1.call-done = (f32[384,1024]{1,0:T(8,128)}, f32[384,1024]{1,0:T(8,128)}) async-done(((f32[384,1024]{1,0:T(8,128)}, f32[384,1024]{1,0:T(8,128)}), (f32[384,1024]{1,0:T(8,128)}, f32[384,1024]{1,0:T(8,128)})) %all-reduce.5.cloned.1.call-update) | async-done | bytes 3145744 | tf_op jit(solution)/shard_map/psum | solution.py:31
  159.1 85.0 %all-reduce.7.cloned.1.call-done = (f32[384,1024]{1,0:T(8,128)}, f32[384,1024]{1,0:T(8,128)}) async-done(((f32[384,1024]{1,0:T(8,128)}, f32[384,1024]{1,0:T(8,128)}), (f32[384,1024]{1,0:T(8,128)}, f32[384,1024]{1,0:T(8,128)})) %all-reduce.7.cloned.1.call-update) | async-done | bytes 3145744 | tf_op jit(solution)/shard_map/psum | solution.py:31
  251.4 18.8 %all-gather = f32[6144,1]{0,1:T(1,128)S(1)} all-gather(f32[384,1]{0,1:T(1,128)S(1)} %get-tuple-element.93), channel_id=2, replica_groups=mesh['row_0'=8,'row_1'=4,'col'=16] {'col'}, dimensions={0}, use_global_device_ids=true | all-gather | bytes 26112 | tf_op jit(solution)/shard_map/all_gather | solution.py:36
  297.7 16.2 %all-gather.1 = f32[6144,1]{0,1:T(1,128)S(1)} all-gather(f32[384,1]{0,1:T(1,128)S(1)} %get-tuple-element.92), channel_id=3, replica_groups=mesh['row_0'=8,'row_1'=4,'col'=16] {'col'}, dimensions={0}, use_global_device_ids=true | all-gather | bytes 26112 | tf_op jit(solution)/shard_map/all_gather | solution.py:36
  316.1 15.7 %all-gather.16 = f32[16,1,768]{2,1,0:T(1,128)S(1)} all-gather(f32[1,1,768]{2,1,0:T(1,128)S(1)} %reshape.407), channel_id=4, replica_groups=mesh['row_0'=8,'row_1'=4,'col'=16] {'col'}, dimensions={0}, use_global_device_ids=true | all-gather | bytes 52224 | tf_op jit(solution)/shard_map/all_gather | solution.py:36
  358.8 16.2 %all-gather.3 = f32[6144,1]{0,1:T(1,128)S(1)} all-gather(f32[384,1]{0,1:T(1,128)S(1)} %get-tuple-element.91), channel_id=5, replica_groups=mesh['row_0'=8,'row_1'=4,'col'=16] {'col'}, dimensions={0}, use_global_device_ids=true | all-gather | bytes 26112 | tf_op jit(solution)/shard_map/all_gather | solution.py:36
  380.1 9.7 %all-to-all-start.5 = ((f32[32,1,768]{2,1,0:T(1,128)}), f32[32,1,768]{2,1,0:T(1,128)S(1)}, u32[]{:S(2)}, u32[]{:S(2)}) async-start(f32[32,1,768]{2,1,0:T(1,128)} %broadcast_in_dim.175), calls=%async_computation.5 | async-start | bytes 196608 | tf_op jit(solution)/shard_map/all_to_all | solution.py:21
  399.0 17.2 %all-gather.17 = f32[16,1,768]{2,1,0:T(1,128)S(1)} all-gather(f32[1,1,768]{2,1,0:T(1,128)S(1)} %reshape.409), channel_id=6, replica_groups=mesh['row_0'=8,'row_1'=4,'col'=16] {'col'}, dimensions={0}, use_global_device_ids=true | all-gather | bytes 52224 | tf_op jit(solution)/shard_map/all_gather | solution.py:36
  437.7 15.9 %all-gather.5 = f32[6144,1]{0,1:T(1,128)S(1)} all-gather(f32[384,1]{0,1:T(1,128)S(1)} %get-tuple-element.90), channel_id=7, replica_groups=mesh['row_0'=8,'row_1'=4,'col'=16] {'col'}, dimensions={0}, use_global_device_ids=true | all-gather | bytes 26112 | tf_op jit(solution)/shard_map/all_gather | solution.py:36
  458.9 9.5 %all-to-all-start.8 = ((f32[32,1,768]{2,1,0:T(1,128)}), f32[32,1,768]{2,1,0:T(1,128)S(1)}, u32[]{:S(2)}, u32[]{:S(2)}) async-start(f32[32,1,768]{2,1,0:T(1,128)} %broadcast_in_dim.178), calls=%async_computation.8 | async-start | bytes 196608 | tf_op jit(solution)/shard_map/all_to_all | solution.py:21
  477.5 17.2 %all-gather.18 = f32[16,1,768]{2,1,0:T(1,128)S(1)} all-gather(f32[1,1,768]{2,1,0:T(1,128)S(1)} %reshape.411), channel_id=8, replica_groups=mesh['row_0'=8,'row_1'=4,'col'=16] {'col'}, dimensions={0}, use_global_device_ids=true | all-gather | bytes 52224 | tf_op jit(solution)/shard_map/all_gather | solution.py:36
  516.2 15.9 %all-gather.7 = f32[6144,1]{0,1:T(1,128)S(1)} all-gather(f32[384,1]{0,1:T(1,128)S(1)} %get-tuple-element.89), channel_id=9, replica_groups=mesh['row_0'=8,'row_1'=4,'col'=16] {'col'}, dimensions={0}, use_global_device_ids=true | all-gather | bytes 26112 | tf_op jit(solution)/shard_map/all_gather | solution.py:36
  556.1 17.2 %all-gather.19 = f32[16,1,768]{2,1,0:T(1,128)S(1)} all-gather(f32[1,1,768]{2,1,0:T(1,128)S(1)} %reshape.413), channel_id=10, replica_groups=mesh['row_0'=8,'row_1'=4,'col'=16] {'col'}, dimensions={0}, use_global_device_ids=true | all-gather | bytes 52224 | tf_op jit(solution)/shard_map/all_gather | solution.py:36
  594.8 15.9 %all-gather.9 = f32[6144,1]{0,1:T(1,128)S(1)} all-gather(f32[384,1]{0,1:T(1,128)S(1)} %get-tuple-element.88), channel_id=11, replica_groups=mesh['row_0'=8,'row_1'=4,'col'=16] {'col'}, dimensions={0}, use_global_device_ids=true | all-gather | bytes 26112 | tf_op jit(solution)/shard_map/all_gather | solution.py:36
  615.9 9.5 %all-to-all-start.14 = ((f32[32,1,768]{2,1,0:T(1,128)}), f32[32,1,768]{2,1,0:T(1,128)S(1)}, u32[]{:S(2)}, u32[]{:S(2)}) async-start(f32[32,1,768]{2,1,0:T(1,128)} %broadcast_in_dim.184), calls=%async_computation.14 | async-start | bytes 196608 | tf_op jit(solution)/shard_map/all_to_all | solution.py:21
  634.5 17.2 %all-gather.20 = f32[16,1,768]{2,1,0:T(1,128)S(1)} all-gather(f32[1,1,768]{2,1,0:T(1,128)S(1)} %reshape.415), channel_id=12, replica_groups=mesh['row_0'=8,'row_1'=4,'col'=16] {'col'}, dimensions={0}, use_global_device_ids=true | all-gather | bytes 52224 | tf_op jit(solution)/shard_map/all_gather | solution.py:36
  673.4 15.9 %all-gather.11 = f32[6144,1]{0,1:T(1,128)S(1)} all-gather(f32[384,1]{0,1:T(1,128)S(1)} %get-tuple-element.87), channel_id=13, replica_groups=mesh['row_0'=8,'row_1'=4,'col'=16] {'col'}, dimensions={0}, use_global_device_ids=true | all-gather | bytes 26112 | tf_op jit(solution)/shard_map/all_gather | solution.py:36
  694.5 9.5 %all-to-all-start.17 = ((f32[32,1,768]{2,1,0:T(1,128)}), f32[32,1,768]{2,1,0:T(1,128)S(1)}, u32[]{:S(2)}, u32[]{:S(2)}) async-start(f32[32,1,768]{2,1,0:T(1,128)} %broadcast_in_dim.187), calls=%async_computation.17 | async-start | bytes 196608 | tf_op jit(solution)/shard_map/all_to_all | solution.py:21
  713.2 17.2 %all-gather.21 = f32[16,1,768]{2,1,0:T(1,128)S(1)} all-gather(f32[1,1,768]{2,1,0:T(1,128)S(1)} %reshape.417), channel_id=14, replica_groups=mesh['row_0'=8,'row_1'=4,'col'=16] {'col'}, dimensions={0}, use_global_device_ids=true | all-gather | bytes 52224 | tf_op jit(solution)/shard_map/all_gather | solution.py:36
  751.9 15.9 %all-gather.13 = f32[6144,1]{0,1:T(1,128)S(1)} all-gather(f32[384,1]{0,1:T(1,128)S(1)} %get-tuple-element.86), channel_id=15, replica_groups=mesh['row_0'=8,'row_1'=4,'col'=16] {'col'}, dimensions={0}, use_global_device_ids=true | all-gather | bytes 26112 | tf_op jit(solution)/shard_map/all_gather | solution.py:36
  791.6 17.2 %all-gather.22 = f32[16,1,768]{2,1,0:T(1,128)S(1)} all-gather(f32[1,1,768]{2,1,0:T(1,128)S(1)} %reshape.419), channel_id=16, replica_groups=mesh['row_0'=8,'row_1'=4,'col'=16] {'col'}, dimensions={0}, use_global_device_ids=true | all-gather | bytes 52224 | tf_op jit(solution)/shard_map/all_gather | solution.py:36
  857.5 18.1 %all-gather.23 = f32[16,1,768]{2,1,0:T(1,128)S(1)} all-gather(f32[1,1,768]{2,1,0:T(1,128)S(1)} %reshape.421), channel_id=17, replica_groups=mesh['row_0'=8,'row_1'=4,'col'=16] {'col'}, dimensions={0}, use_global_device_ids=true | all-gather | bytes 52224 | tf_op jit(solution)/shard_map/all_gather | solution.py:36
  (303 shorter events, 327.1 us)
Async XLA Ops:
  9.4 50.3 %all-to-all-start = ((f32[16,24,1024]{2,1,0:T(8,128)}), f32[16,24,1024]{2,1,0:T(8,128)S(1)}, u32[]{:S(2)}, u32[]{:S(2)}) async-start(f32[16,24,1024]{2,1,0:T(8,128)} %broadcast_in_dim.166), calls=%async_computation | async-start | bytes 3145728 | tf_op jit(solution)/shard_map/all_to_all | solution.py:21
  21.2 134.5 %all-reduce.5.cloned.1.call-start = ((), (), s32[]{:S(2)}) async-start(), calls=%async_computation.25 | async-start | bytes 6291456 | tf_op jit(solution)/shard_map/psum | solution.py:31
  61.8 182.4 %all-reduce.7.cloned.1.call-start = ((), (), s32[]{:S(2)}) async-start(), calls=%async_computation.26 | async-start | bytes 6291456 | tf_op jit(solution)/shard_map/psum | solution.py:31
  272.4 16.4 %all-to-all-start.1 = ((f32[32,1,26]{2,1,0:T(1,128)}), f32[32,1,26]{2,1,0:T(1,128)S(1)}, u32[]{:S(2)}, u32[]{:S(2)}) async-start(f32[32,1,26]{2,1,0:T(1,128)} %broadcast_in_dim.171), calls=%async_computation.1 | async-start | bytes 32768 | tf_op jit(solution)/shard_map/all_to_all | solution.py:21
  293.9 22.2 %all-to-all-start.2 = ((f32[32,1,768]{2,1,0:T(1,128)}), f32[32,1,768]{2,1,0:T(1,128)S(1)}, u32[]{:S(2)}, u32[]{:S(2)}) async-start(f32[32,1,768]{2,1,0:T(1,128)} %broadcast_in_dim.172), calls=%async_computation.2 | async-start | bytes 196608 | tf_op jit(solution)/shard_map/all_to_all | solution.py:21
  333.8 18.0 %all-to-all-start.3 = ((f32[32,1,10]{2,1,0:T(1,128)}), f32[32,1,10]{2,1,0:T(1,128)S(1)}, u32[]{:S(2)}, u32[]{:S(2)}) async-start(f32[32,1,10]{2,1,0:T(1,128)} %broadcast_in_dim.173), calls=%async_computation.3 | async-start | bytes 32768 | tf_op jit(solution)/shard_map/all_to_all | solution.py:21
  355.0 20.1 %all-to-all-start.4 = ((f32[32,1,26]{2,1,0:T(1,128)}), f32[32,1,26]{2,1,0:T(1,128)S(1)}, u32[]{:S(2)}, u32[]{:S(2)}) async-start(f32[32,1,26]{2,1,0:T(1,128)} %broadcast_in_dim.174), calls=%async_computation.4 | async-start | bytes 32768 | tf_op jit(solution)/shard_map/all_to_all | solution.py:21
  380.1 18.8 %all-to-all-start.5 = ((f32[32,1,768]{2,1,0:T(1,128)}), f32[32,1,768]{2,1,0:T(1,128)S(1)}, u32[]{:S(2)}, u32[]{:S(2)}) async-start(f32[32,1,768]{2,1,0:T(1,128)} %broadcast_in_dim.175), calls=%async_computation.5 | async-start | bytes 196608 | tf_op jit(solution)/shard_map/all_to_all | solution.py:21
  418.3 12.4 %all-to-all-start.6 = ((f32[32,1,10]{2,1,0:T(1,128)}), f32[32,1,10]{2,1,0:T(1,128)S(1)}, u32[]{:S(2)}, u32[]{:S(2)}) async-start(f32[32,1,10]{2,1,0:T(1,128)} %broadcast_in_dim.176), calls=%async_computation.6 | async-start | bytes 32768 | tf_op jit(solution)/shard_map/all_to_all | solution.py:21
  433.8 19.8 %all-to-all-start.7 = ((f32[32,1,26]{2,1,0:T(1,128)}), f32[32,1,26]{2,1,0:T(1,128)S(1)}, u32[]{:S(2)}, u32[]{:S(2)}) async-start(f32[32,1,26]{2,1,0:T(1,128)} %broadcast_in_dim.177), calls=%async_computation.7 | async-start | bytes 32768 | tf_op jit(solution)/shard_map/all_to_all | solution.py:21
  458.9 18.6 %all-to-all-start.8 = ((f32[32,1,768]{2,1,0:T(1,128)}), f32[32,1,768]{2,1,0:T(1,128)S(1)}, u32[]{:S(2)}, u32[]{:S(2)}) async-start(f32[32,1,768]{2,1,0:T(1,128)} %broadcast_in_dim.178), calls=%async_computation.8 | async-start | bytes 196608 | tf_op jit(solution)/shard_map/all_to_all | solution.py:21
  496.8 12.4 %all-to-all-start.9 = ((f32[32,1,10]{2,1,0:T(1,128)}), f32[32,1,10]{2,1,0:T(1,128)S(1)}, u32[]{:S(2)}, u32[]{:S(2)}) async-start(f32[32,1,10]{2,1,0:T(1,128)} %broadcast_in_dim.179), calls=%async_computation.9 | async-start | bytes 32768 | tf_op jit(solution)/shard_map/all_to_all | solution.py:21
  512.4 19.8 %all-to-all-start.10 = ((f32[32,1,26]{2,1,0:T(1,128)}), f32[32,1,26]{2,1,0:T(1,128)S(1)}, u32[]{:S(2)}, u32[]{:S(2)}) async-start(f32[32,1,26]{2,1,0:T(1,128)} %broadcast_in_dim.180), calls=%async_computation.10 | async-start | bytes 32768 | tf_op jit(solution)/shard_map/all_to_all | solution.py:21
  537.4 18.6 %all-to-all-start.11 = ((f32[32,1,768]{2,1,0:T(1,128)}), f32[32,1,768]{2,1,0:T(1,128)S(1)}, u32[]{:S(2)}, u32[]{:S(2)}) async-start(f32[32,1,768]{2,1,0:T(1,128)} %broadcast_in_dim.181), calls=%async_computation.11 | async-start | bytes 196608 | tf_op jit(solution)/shard_map/all_to_all | solution.py:21
  590.9 19.8 %all-to-all-start.13 = ((f32[32,1,26]{2,1,0:T(1,128)}), f32[32,1,26]{2,1,0:T(1,128)S(1)}, u32[]{:S(2)}, u32[]{:S(2)}) async-start(f32[32,1,26]{2,1,0:T(1,128)} %broadcast_in_dim.183), calls=%async_computation.13 | async-start | bytes 32768 | tf_op jit(solution)/shard_map/all_to_all | solution.py:21
  615.9 18.6 %all-to-all-start.14 = ((f32[32,1,768]{2,1,0:T(1,128)}), f32[32,1,768]{2,1,0:T(1,128)S(1)}, u32[]{:S(2)}, u32[]{:S(2)}) async-start(f32[32,1,768]{2,1,0:T(1,128)} %broadcast_in_dim.184), calls=%async_computation.14 | async-start | bytes 196608 | tf_op jit(solution)/shard_map/all_to_all | solution.py:21
  669.4 20.0 %all-to-all-start.16 = ((f32[32,1,26]{2,1,0:T(1,128)}), f32[32,1,26]{2,1,0:T(1,128)S(1)}, u32[]{:S(2)}, u32[]{:S(2)}) async-start(f32[32,1,26]{2,1,0:T(1,128)} %broadcast_in_dim.186), calls=%async_computation.16 | async-start | bytes 32768 | tf_op jit(solution)/shard_map/all_to_all | solution.py:21
  694.5 18.6 %all-to-all-start.17 = ((f32[32,1,768]{2,1,0:T(1,128)}), f32[32,1,768]{2,1,0:T(1,128)S(1)}, u32[]{:S(2)}, u32[]{:S(2)}) async-start(f32[32,1,768]{2,1,0:T(1,128)} %broadcast_in_dim.187), calls=%async_computation.17 | async-start | bytes 196608 | tf_op jit(solution)/shard_map/all_to_all | solution.py:21
  732.4 12.4 %all-to-all-start.18 = ((f32[32,1,10]{2,1,0:T(1,128)}), f32[32,1,10]{2,1,0:T(1,128)S(1)}, u32[]{:S(2)}, u32[]{:S(2)}) async-start(f32[32,1,10]{2,1,0:T(1,128)} %broadcast_in_dim.188), calls=%async_computation.18 | async-start | bytes 32768 | tf_op jit(solution)/shard_map/all_to_all | solution.py:21
  748.0 19.8 %all-to-all-start.19 = ((f32[32,1,26]{2,1,0:T(1,128)}), f32[32,1,26]{2,1,0:T(1,128)S(1)}, u32[]{:S(2)}, u32[]{:S(2)}) async-start(f32[32,1,26]{2,1,0:T(1,128)} %broadcast_in_dim.189), calls=%async_computation.19 | async-start | bytes 32768 | tf_op jit(solution)/shard_map/all_to_all | solution.py:21
  773.0 18.6 %all-to-all-start.20 = ((f32[32,1,768]{2,1,0:T(1,128)}), f32[32,1,768]{2,1,0:T(1,128)S(1)}, u32[]{:S(2)}, u32[]{:S(2)}) async-start(f32[32,1,768]{2,1,0:T(1,128)} %broadcast_in_dim.190), calls=%async_computation.20 | async-start | bytes 196608 | tf_op jit(solution)/shard_map/all_to_all | solution.py:21
  826.6 12.5 %all-to-all-start.22 = ((f32[32,1,26]{2,1,0:T(1,128)}), f32[32,1,26]{2,1,0:T(1,128)S(1)}, u32[]{:S(2)}, u32[]{:S(2)}) async-start(f32[32,1,26]{2,1,0:T(1,128)} %broadcast_in_dim.192), calls=%async_computation.22 | async-start | bytes 32768 | tf_op jit(solution)/shard_map/all_to_all | solution.py:21
  844.4 13.0 %all-to-all-start.23 = ((f32[32,1,768]{2,1,0:T(1,128)}), f32[32,1,768]{2,1,0:T(1,128)S(1)}, u32[]{:S(2)}, u32[]{:S(2)}) async-start(f32[32,1,768]{2,1,0:T(1,128)} %broadcast_in_dim.193), calls=%async_computation.23 | async-start | bytes 196608 | tf_op jit(solution)/shard_map/all_to_all | solution.py:21
  877.7 13.5 %all-to-all-start.24 = ((f32[32,1,10]{2,1,0:T(1,128)}), f32[32,1,10]{2,1,0:T(1,128)S(1)}, u32[]{:S(2)}, u32[]{:S(2)}) async-start(f32[32,1,10]{2,1,0:T(1,128)} %broadcast_in_dim.194), calls=%async_computation.24 | async-start | bytes 32768 | tf_op jit(solution)/shard_map/all_to_all | solution.py:21
  (5 other events, 125.6 us)
Sparse Core Ops, SparseCore 0:
  61.9 93.7 all-reduce.4
  158.1 85.9 all-reduce.6
where the time goes:
time: 901 us; the launch traced here: 899 us
  waiting for transfers between devices  356 us (40%)
  blocking collectives  268 us (30%)
  starting transfers between devices  149 us (17%)
  between operations  36.2 us (4%)
  local copies, waits for them, and re-layouts  33.9 us (4%)
  other arithmetic  30.2 us (3%)
  matrix products  25.4 us (3%)
    all_gather x16, blocking collectives, picked(): lax.all_gather(value, axis)  268 us
    psum x2, waiting for transfers between devices, spread(): value = lax.psum(value, axis)  179 us
    all_to_all x25, waiting for transfers between devices, sent_to_all(): return lax.all_to_all(copies, axis, split_axis=0, concat_axis=0, tiled=True)  177 us
    all_to_all x25, starting transfers between devices, sent_to_all(): return lax.all_to_all(copies, axis, split_axis=0, concat_axis=0, tiled=True)  149 us
  transfers between devices with their start and end apart: 27, of which 20 were waited for; matrix products, arithmetic and copies ran while one was open for 2% of the time, Pallas kernels for 0%

commit v1 on v0

--- a/solution.py
+++ b/solution.py
@@ -28,7 +28,7 @@
 def spread(value, axes, root):
     value = jnp.where(lax.axis_index(axes) == root, value, jnp.zeros_like(value))
     for axis in axes:
-        value = lax.psum(value, axis)
+        value = jnp.sum(lax.all_gather(value, axis), axis=0)
     return value
 
 

time: 901 us -> 1140 us (1.27)
  waiting for transfers between devices: 356 us -> 570 us
  other arithmetic: 30.2 us -> 54.7 us
    all_gather x0 -> x4, waiting for transfers between devices: none -> 392 us  [spread(): value = jnp.sum(lax.all_gather(value, axis), axis=0)]
    psum x2 -> x0, waiting for transfers between devices: 179 us -> none  [spread(): value = lax.psum(value, axis)]
    reduce_sum x0 -> x4, other arithmetic: none -> 24.4 us  [spread(): value = jnp.sum(lax.all_gather(value, axis), axis=0)]
  transfers between devices with their start and end apart: 27 -> 29, of which waited for: 20 -> 22; matrix products, arithmetic and copies ran while one was open for 2% -> 3% of each run, Pallas kernels for 0% -> 0%
where the time goes in v1:
time: 1140 us
  waiting for transfers between devices  570 us (50%)
  blocking collectives  269 us (24%)
  starting transfers between devices  150 us (13%)
  other arithmetic  54.7 us (5%)
  between operations  36.1 us (3%)
  local copies, waits for them, and re-layouts  33.9 us (3%)
  matrix products  25.4 us (2%)
    all_gather x4, waiting for transfers between devices, spread(): value = jnp.sum(lax.all_gather(value, axis), axis=0)  392 us
    all_gather x16, blocking collectives, picked(): lax.all_gather(value, axis)  269 us
    all_to_all x25, waiting for transfers between devices, sent_to_all(): return lax.all_to_all(copies, axis, split_axis=0, concat_axis=0, tiled=True)  177 us
    all_to_all x25, starting transfers between devices, sent_to_all(): return lax.all_to_all(copies, axis, split_axis=0, concat_axis=0, tiled=True)  149 us
    reduce_sum x4, other arithmetic, spread(): value = jnp.sum(lax.all_gather(value, axis), axis=0)  24.4 us
  transfers between devices with their start and end apart: 29, of which 22 were waited for; matrix products, arithmetic and copies ran while one was open for 3% of the time, Pallas kernels for 0%

profile of v1, /device:TPU:1, one launch (start us, length us, event | category | flops | bytes accessed | tf_op | source)
XLA Modules:
  0.0 1138.3 jit_solution(15149874602265984991)
XLA Ops:
  9.4 11.8 %all-to-all-start = ((f32[16,24,1024]{2,1,0:T(8,128)}), f32[16,24,1024]{2,1,0:T(8,128)S(1)}, u32[]{:S(2)}, u32[]{:S(2)}) async-start(f32[16,24,1024]{2,1,0:T(8,128)} %broadcast_in_dim.166), calls=%async_computation | async-start | bytes 3145728 | tf_op jit(solution)/shard_map/all_to_all | solution.py:21
  21.3 38.5 %all-to-all-done = f32[16,24,1024]{2,1,0:T(8,128)S(1)} async-done(((f32[16,24,1024]{2,1,0:T(8,128)}), f32[16,24,1024]{2,1,0:T(8,128)S(1)}, u32[]{:S(2)}, u32[]{:S(2)}) %all-to-all-start) | async-done | bytes 1572896 | tf_op jit(solution)/shard_map/all_to_all | solution.py:21
  62.7 132.7 %all-gather.31.cloned.1.call-done = f32[8,384,1024]{2,1,0:T(8,128)} async-done(((f32[1,384,1024]{2,1,0:T(8,128)}), f32[8,384,1024]{2,1,0:T(8,128)}) %all-gather.31.cloned.1.call-update) | async-done | bytes 12582928 | tf_op jit(solution)/shard_map/all_gather | solution.py:31
  203.3 128.9 %all-gather.33.cloned.1.call-done = f32[8,384,1024]{2,1,0:T(8,128)} async-done(((f32[1,384,1024]{2,1,0:T(8,128)}), f32[8,384,1024]{2,1,0:T(8,128)}) %all-gather.33.cloned.1.call-update) | async-done | bytes 12582928 | tf_op jit(solution)/shard_map/all_gather | solution.py:31
  343.1 61.3 %all-gather.35.cloned.1.call-done = f32[1536,1024]{1,0:T(8,128)} async-done(((f32[384,1024]{1,0:T(8,128)}), f32[1536,1024]{1,0:T(8,128)}) %all-gather.35.cloned.1.call-update) | async-done | bytes 6291472 | tf_op jit(solution)/shard_map/all_gather | solution.py:31
  409.2 68.9 %all-gather.37.cloned.1.call-done = f32[1536,1024]{1,0:T(8,128)} async-done(((f32[384,1024]{1,0:T(8,128)}), f32[1536,1024]{1,0:T(8,128)}) %all-gather.37.cloned.1.call-update) | async-done | bytes 6291472 | tf_op jit(solution)/shard_map/all_gather | solution.py:31
  490.2 18.8 %all-gather.2 = f32[6144,1]{0,1:T(1,128)S(1)} all-gather(f32[384,1]{0,1:T(1,128)S(1)} %get-tuple-element.89), channel_id=4, replica_groups=mesh['row_0'=8,'row_1'=4,'col'=16] {'col'}, dimensions={0}, use_global_device_ids=true | all-gather | bytes 26112 | tf_op jit(solution)/shard_map/all_gather | solution.py:36
  537.3 16.2 %all-gather.3 = f32[6144,1]{0,1:T(1,128)S(1)} all-gather(f32[384,1]{0,1:T(1,128)S(1)} %get-tuple-element.88), channel_id=5, replica_groups=mesh['row_0'=8,'row_1'=4,'col'=16] {'col'}, dimensions={0}, use_global_device_ids=true | all-gather | bytes 26112 | tf_op jit(solution)/shard_map/all_gather | solution.py:36
  555.7 15.8 %all-gather.18 = f32[16,1,768]{2,1,0:T(1,128)S(1)} all-gather(f32[1,1,768]{2,1,0:T(1,128)S(1)} %reshape.435), channel_id=6, replica_groups=mesh['row_0'=8,'row_1'=4,'col'=16] {'col'}, dimensions={0}, use_global_device_ids=true | all-gather | bytes 52224 | tf_op jit(solution)/shard_map/all_gather | solution.py:36
  598.6 16.2 %all-gather.5 = f32[6144,1]{0,1:T(1,128)S(1)} all-gather(f32[384,1]{0,1:T(1,128)S(1)} %get-tuple-element.87), channel_id=7, replica_groups=mesh['row_0'=8,'row_1'=4,'col'=16] {'col'}, dimensions={0}, use_global_device_ids=true | all-gather | bytes 26112 | tf_op jit(solution)/shard_map/all_gather | solution.py:36
  638.6 17.2 %all-gather.19 = f32[16,1,768]{2,1,0:T(1,128)S(1)} all-gather(f32[1,1,768]{2,1,0:T(1,128)S(1)} %reshape.437), channel_id=8, replica_groups=mesh['row_0'=8,'row_1'=4,'col'=16] {'col'}, dimensions={0}, use_global_device_ids=true | all-gather | bytes 52224 | tf_op jit(solution)/shard_map/all_gather | solution.py:36
  677.3 15.9 %all-gather.7 = f32[6144,1]{0,1:T(1,128)S(1)} all-gather(f32[384,1]{0,1:T(1,128)S(1)} %get-tuple-element.86), channel_id=9, replica_groups=mesh['row_0'=8,'row_1'=4,'col'=16] {'col'}, dimensions={0}, use_global_device_ids=true | all-gather | bytes 26112 | tf_op jit(solution)/shard_map/all_gather | solution.py:36
  717.1 17.2 %all-gather.20 = f32[16,1,768]{2,1,0:T(1,128)S(1)} all-gather(f32[1,1,768]{2,1,0:T(1,128)S(1)} %reshape.439), channel_id=10, replica_groups=mesh['row_0'=8,'row_1'=4,'col'=16] {'col'}, dimensions={0}, use_global_device_ids=true | all-gather | bytes 52224 | tf_op jit(solution)/shard_map/all_gather | solution.py:36
  755.8 15.9 %all-gather.9 = f32[6144,1]{0,1:T(1,128)S(1)} all-gather(f32[384,1]{0,1:T(1,128)S(1)} %get-tuple-element.85), channel_id=11, replica_groups=mesh['row_0'=8,'row_1'=4,'col'=16] {'col'}, dimensions={0}, use_global_device_ids=true | all-gather | bytes 26112 | tf_op jit(solution)/shard_map/all_gather | solution.py:36
  795.7 17.2 %all-gather.21 = f32[16,1,768]{2,1,0:T(1,128)S(1)} all-gather(f32[1,1,768]{2,1,0:T(1,128)S(1)} %reshape.441), channel_id=12, replica_groups=mesh['row_0'=8,'row_1'=4,'col'=16] {'col'}, dimensions={0}, use_global_device_ids=true | all-gather | bytes 52224 | tf_op jit(solution)/shard_map/all_gather | solution.py:36
  834.4 16.2 %all-gather.11 = f32[6144,1]{0,1:T(1,128)S(1)} all-gather(f32[384,1]{0,1:T(1,128)S(1)} %get-tuple-element.84), channel_id=13, replica_groups=mesh['row_0'=8,'row_1'=4,'col'=16] {'col'}, dimensions={0}, use_global_device_ids=true | all-gather | bytes 26112 | tf_op jit(solution)/shard_map/all_gather | solution.py:36
  874.3 17.2 %all-gather.22 = f32[16,1,768]{2,1,0:T(1,128)S(1)} all-gather(f32[1,1,768]{2,1,0:T(1,128)S(1)} %reshape.443), channel_id=14, replica_groups=mesh['row_0'=8,'row_1'=4,'col'=16] {'col'}, dimensions={0}, use_global_device_ids=true | all-gather | bytes 52224 | tf_op jit(solution)/shard_map/all_gather | solution.py:36
  913.0 15.9 %all-gather.13 = f32[6144,1]{0,1:T(1,128)S(1)} all-gather(f32[384,1]{0,1:T(1,128)S(1)} %get-tuple-element.83), channel_id=15, replica_groups=mesh['row_0'=8,'row_1'=4,'col'=16] {'col'}, dimensions={0}, use_global_device_ids=true | all-gather | bytes 26112 | tf_op jit(solution)/shard_map/all_gather | solution.py:36
  934.1 9.5 all-to-all-start.17
  952.7 17.2 %all-gather.23 = f32[16,1,768]{2,1,0:T(1,128)S(1)} all-gather(f32[1,1,768]{2,1,0:T(1,128)S(1)} %reshape.445), channel_id=16, replica_groups=mesh['row_0'=8,'row_1'=4,'col'=16] {'col'}, dimensions={0}, use_global_device_ids=true | all-gather | bytes 52224 | tf_op jit(solution)/shard_map/all_gather | solution.py:36
  991.5 15.9 %all-gather.15 = f32[6144,1]{0,1:T(1,128)S(1)} all-gather(f32[384,1]{0,1:T(1,128)S(1)} %get-tuple-element.82), channel_id=17, replica_groups=mesh['row_0'=8,'row_1'=4,'col'=16] {'col'}, dimensions={0}, use_global_device_ids=true | all-gather | bytes 26112 | tf_op jit(solution)/shard_map/all_gather | solution.py:36
  1012.5 9.5 all-to-all-start.20
  1031.2 17.2 %all-gather.24 = f32[16,1,768]{2,1,0:T(1,128)S(1)} all-gather(f32[1,1,768]{2,1,0:T(1,128)S(1)} %reshape.447), channel_id=18, replica_groups=mesh['row_0'=8,'row_1'=4,'col'=16] {'col'}, dimensions={0}, use_global_device_ids=true | all-gather | bytes 52224 | tf_op jit(solution)/shard_map/all_gather | solution.py:36
  1097.1 18.1 %all-gather.25 = f32[16,1,768]{2,1,0:T(1,128)S(1)} all-gather(f32[1,1,768]{2,1,0:T(1,128)S(1)} %reshape.449), channel_id=19, replica_groups=mesh['row_0'=8,'row_1'=4,'col'=16] {'col'}, dimensions={0}, use_global_device_ids=true | all-gather | bytes 52224 | tf_op jit(solution)/shard_map/all_gather | solution.py:36
  (313 shorter events, 372.5 us)
Async XLA Ops:
  9.4 50.3 %all-to-all-start = ((f32[16,24,1024]{2,1,0:T(8,128)}), f32[16,24,1024]{2,1,0:T(8,128)S(1)}, u32[]{:S(2)}, u32[]{:S(2)}) async-start(f32[16,24,1024]{2,1,0:T(8,128)} %broadcast_in_dim.166), calls=%async_computation | async-start | bytes 3145728 | tf_op jit(solution)/shard_map/all_to_all | solution.py:21
  21.2 174.2 %all-gather.31.cloned.1.call-start = ((), (), s32[]{:S(2)}) async-start(), calls=%async_computation.25 | async-start | bytes 14155776 | tf_op jit(solution)/shard_map/all_gather | solution.py:31
  61.9 270.4 %all-gather.33.cloned.1.call-start = ((), (), s32[]{:S(2)}) async-start(), calls=%async_computation.26 | async-start | bytes 14155776 | tf_op jit(solution)/shard_map/all_gather | solution.py:31
  62.7 341.7 %all-gather.35.cloned.1.call-start = ((), (), s32[]{:S(2)}) async-start(), calls=%async_computation.27 | async-start | bytes 7864320 | tf_op jit(solution)/shard_map/all_gather | solution.py:31
  202.8 275.2 %all-gather.37.cloned.1.call-start = ((), (), s32[]{:S(2)}) async-start(), calls=%async_computation.28 | async-start | bytes 7864320 | tf_op jit(solution)/shard_map/all_gather | solution.py:31
  511.2 17.2 %all-to-all-start.1 = ((f32[32,1,26]{2,1,0:T(1,128)}), f32[32,1,26]{2,1,0:T(1,128)S(1)}, u32[]{:S(2)}, u32[]{:S(2)}) async-start(f32[32,1,26]{2,1,0:T(1,128)} %broadcast_in_dim.171), calls=%async_computation.1 | async-start | bytes 32768 | tf_op jit(solution)/shard_map/all_to_all | solution.py:21
  533.5 22.2 %all-to-all-start.2 = ((f32[32,1,768]{2,1,0:T(1,128)}), f32[32,1,768]{2,1,0:T(1,128)S(1)}, u32[]{:S(2)}, u32[]{:S(2)}) async-start(f32[32,1,768]{2,1,0:T(1,128)} %broadcast_in_dim.172), calls=%async_computation.2 | async-start | bytes 196608 | tf_op jit(solution)/shard_map/all_to_all | solution.py:21
  573.6 18.0 %all-to-all-start.3 = ((f32[32,1,10]{2,1,0:T(1,128)}), f32[32,1,10]{2,1,0:T(1,128)S(1)}, u32[]{:S(2)}, u32[]{:S(2)}) async-start(f32[32,1,10]{2,1,0:T(1,128)} %broadcast_in_dim.173), calls=%async_computation.3 | async-start | bytes 32768 | tf_op jit(solution)/shard_map/all_to_all | solution.py:21
  594.8 20.0 %all-to-all-start.4 = ((f32[32,1,26]{2,1,0:T(1,128)}), f32[32,1,26]{2,1,0:T(1,128)S(1)}, u32[]{:S(2)}, u32[]{:S(2)}) async-start(f32[32,1,26]{2,1,0:T(1,128)} %broadcast_in_dim.174), calls=%async_computation.4 | async-start | bytes 32768 | tf_op jit(solution)/shard_map/all_to_all | solution.py:21
  619.9 18.6 %all-to-all-start.5 = ((f32[32,1,768]{2,1,0:T(1,128)}), f32[32,1,768]{2,1,0:T(1,128)S(1)}, u32[]{:S(2)}, u32[]{:S(2)}) async-start(f32[32,1,768]{2,1,0:T(1,128)} %broadcast_in_dim.175), calls=%async_computation.5 | async-start | bytes 196608 | tf_op jit(solution)/shard_map/all_to_all | solution.py:21
  673.4 19.8 %all-to-all-start.7 = ((f32[32,1,26]{2,1,0:T(1,128)}), f32[32,1,26]{2,1,0:T(1,128)S(1)}, u32[]{:S(2)}, u32[]{:S(2)}) async-start(f32[32,1,26]{2,1,0:T(1,128)} %broadcast_in_dim.177), calls=%async_computation.7 | async-start | bytes 32768 | tf_op jit(solution)/shard_map/all_to_all | solution.py:21
  698.5 18.6 %all-to-all-start.8 = ((f32[32,1,768]{2,1,0:T(1,128)}), f32[32,1,768]{2,1,0:T(1,128)S(1)}, u32[]{:S(2)}, u32[]{:S(2)}) async-start(f32[32,1,768]{2,1,0:T(1,128)} %broadcast_in_dim.178), calls=%async_computation.8 | async-start | bytes 196608 | tf_op jit(solution)/shard_map/all_to_all | solution.py:21
  752.0 19.8 %all-to-all-start.10 = ((f32[32,1,26]{2,1,0:T(1,128)}), f32[32,1,26]{2,1,0:T(1,128)S(1)}, u32[]{:S(2)}, u32[]{:S(2)}) async-start(f32[32,1,26]{2,1,0:T(1,128)} %broadcast_in_dim.180), calls=%async_computation.10 | async-start | bytes 32768 | tf_op jit(solution)/shard_map/all_to_all | solution.py:21
  777.0 18.6 %all-to-all-start.11 = ((f32[32,1,768]{2,1,0:T(1,128)}), f32[32,1,768]{2,1,0:T(1,128)S(1)}, u32[]{:S(2)}, u32[]{:S(2)}) async-start(f32[32,1,768]{2,1,0:T(1,128)} %broadcast_in_dim.181), calls=%async_computation.11 | async-start | bytes 196608 | tf_op jit(solution)/shard_map/all_to_all | solution.py:21
  830.5 20.0 %all-to-all-start.13 = ((f32[32,1,26]{2,1,0:T(1,128)}), f32[32,1,26]{2,1,0:T(1,128)S(1)}, u32[]{:S(2)}, u32[]{:S(2)}) async-start(f32[32,1,26]{2,1,0:T(1,128)} %broadcast_in_dim.183), calls=%async_computation.13 | async-start | bytes 32768 | tf_op jit(solution)/shard_map/all_to_all | solution.py:21
  855.7 18.6 %all-to-all-start.14 = ((f32[32,1,768]{2,1,0:T(1,128)}), f32[32,1,768]{2,1,0:T(1,128)S(1)}, u32[]{:S(2)}, u32[]{:S(2)}) async-start(f32[32,1,768]{2,1,0:T(1,128)} %broadcast_in_dim.184), calls=%async_computation.14 | async-start | bytes 196608 | tf_op jit(solution)/shard_map/all_to_all | solution.py:21
  909.2 19.8 %all-to-all-start.16 = ((f32[32,1,26]{2,1,0:T(1,128)}), f32[32,1,26]{2,1,0:T(1,128)S(1)}, u32[]{:S(2)}, u32[]{:S(2)}) async-start(f32[32,1,26]{2,1,0:T(1,128)} %broadcast_in_dim.186), calls=%async_computation.16 | async-start | bytes 32768 | tf_op jit(solution)/shard_map/all_to_all | solution.py:21
  934.1 18.6 %all-to-all-start.17 = ((f32[32,1,768]{2,1,0:T(1,128)}), f32[32,1,768]{2,1,0:T(1,128)S(1)}, u32[]{:S(2)}, u32[]{:S(2)}) async-start(f32[32,1,768]{2,1,0:T(1,128)} %broadcast_in_dim.187), calls=%async_computation.17 | async-start | bytes 196608 | tf_op jit(solution)/shard_map/all_to_all | solution.py:21
  987.6 19.8 %all-to-all-start.19 = ((f32[32,1,26]{2,1,0:T(1,128)}), f32[32,1,26]{2,1,0:T(1,128)S(1)}, u32[]{:S(2)}, u32[]{:S(2)}) async-start(f32[32,1,26]{2,1,0:T(1,128)} %broadcast_in_dim.189), calls=%async_computation.19 | async-start | bytes 32768 | tf_op jit(solution)/shard_map/all_to_all | solution.py:21
  1012.5 18.6 %all-to-all-start.20 = ((f32[32,1,768]{2,1,0:T(1,128)}), f32[32,1,768]{2,1,0:T(1,128)S(1)}, u32[]{:S(2)}, u32[]{:S(2)}) async-start(f32[32,1,768]{2,1,0:T(1,128)} %broadcast_in_dim.190), calls=%async_computation.20 | async-start | bytes 196608 | tf_op jit(solution)/shard_map/all_to_all | solution.py:21
  1050.5 12.4 %all-to-all-start.21 = ((f32[32,1,10]{2,1,0:T(1,128)}), f32[32,1,10]{2,1,0:T(1,128)S(1)}, u32[]{:S(2)}, u32[]{:S(2)}) async-start(f32[32,1,10]{2,1,0:T(1,128)} %broadcast_in_dim.191), calls=%async_computation.21 | async-start | bytes 32768 | tf_op jit(solution)/shard_map/all_to_all | solution.py:21
  1066.1 12.5 %all-to-all-start.22 = ((f32[32,1,26]{2,1,0:T(1,128)}), f32[32,1,26]{2,1,0:T(1,128)S(1)}, u32[]{:S(2)}, u32[]{:S(2)}) async-start(f32[32,1,26]{2,1,0:T(1,128)} %broadcast_in_dim.192), calls=%async_computation.22 | async-start | bytes 32768 | tf_op jit(solution)/shard_map/all_to_all | solution.py:21
  1084.0 13.0 %all-to-all-start.23 = ((f32[32,1,768]{2,1,0:T(1,128)}), f32[32,1,768]{2,1,0:T(1,128)S(1)}, u32[]{:S(2)}, u32[]{:S(2)}) async-start(f32[32,1,768]{2,1,0:T(1,128)} %broadcast_in_dim.193), calls=%async_computation.23 | async-start | bytes 196608 | tf_op jit(solution)/shard_map/all_to_all | solution.py:21
  1117.2 13.5 %all-to-all-start.24 = ((f32[32,1,10]{2,1,0:T(1,128)}), f32[32,1,10]{2,1,0:T(1,128)S(1)}, u32[]{:S(2)}, u32[]{:S(2)}) async-start(f32[32,1,10]{2,1,0:T(1,128)} %broadcast_in_dim.194), calls=%async_computation.24 | async-start | bytes 32768 | tf_op jit(solution)/shard_map/all_to_all | solution.py:21
  (7 other events, 68.0 us)
Sparse Core Ops, SparseCore 0:
  62.0 133.3 all-gather.30
  197.5 134.7 all-gather.32
  334.4 69.9 all-gather.34
  406.4 71.6 all-gather.36
